TPU v7x, 32 devices: a whole 2x2x4 slice. The times are simulated.
32 devices in a mesh: dp: 4 (over x, core), wide: 8 (over z, y).
Axes of the slice: x: 2, y: 2, z: 4, core: 2. Of those that a mesh axis runs over, the one named last changes fastest.
Arguments:
- streams: float32 [4, 4096, 2048], P(None, 'dp', 'wide'), may hold values from -8 to 8
- cotangent: float32 [4, 4096, 2048], P(None, 'dp', 'wide'), may hold values from -6 to 6
- w_query: bfloat16 [2048, 2048], P('dp', 'wide'), may hold values from -2 to 2
- w_key: bfloat16 [2048, 2048], P('dp', 'wide'), may hold values from -0.125 to 0.125
- w_value: bfloat16 [2048, 2048], P('dp', 'wide'), may hold values from -0.125 to 0.125
- w_out: bfloat16 [2048, 2048], P('wide', 'dp'), may hold values from -1 to 1
- w_gate: bfloat16 [2048, 8192], P('dp', 'wide'), may hold values from -0.125 to 0.125
- w_up: bfloat16 [2048, 8192], P('dp', 'wide'), may hold values from -0.125 to 0.125
- w_down: bfloat16 [8192, 2048], P('wide', 'dp'), may hold values from -0.0625 to 0.0625
- hyper: float32 [2, 4, 6], replicated, may hold values from 0.1 to 0.6
- doc_ids: int32 [4, 1024], P('dp'), may hold values from 0 to 3, never falling along the last dimension, each value on 1 to 512 neighbouring positions
- span_starts: int32 [4, 2], P('dp'), may hold values from 0 to 768, as said below
- span_lengths: int32 [4, 2], P('dp'), may hold values from 64 to 256
Outputs:
- out_streams: float32 [4, 4096, 2048], P(None, 'dp', 'wide')
- d_streams: float32 [4, 4096, 2048], P(None, 'dp', 'wide')
- grad_query: float32 [2048, 2048], P('dp', 'wide')
- grad_key: float32 [2048, 2048], P('dp', 'wide')
- grad_value: float32 [2048, 2048], P('dp', 'wide')
- grad_out: float32 [2048, 2048], P('wide', 'dp')
- grad_gate: float32 [2048, 8192], P('dp', 'wide')
- grad_up: float32 [2048, 8192], P('dp', 'wide')
- grad_down: float32 [8192, 2048], P('wide', 'dp')
- grad_hyper: float32 [2, 4, 6], replicated
- clip_scale: float32 [16], P('wide')
- query_clipped: float32 [2048, 2048], P('dp', 'wide')
- key_clipped: float32 [2048, 2048], P('dp', 'wide')
Inputs may be any that keep to these rules, and one draw needn't show every extreme that they name: `doc_ids`: each row's document numbers never fall; every document holds 1 to 512 tokens, and one holds exactly 512. `span_starts`: span k of a sequence starts and ends inside the k-th of 2 equal regions of the sequence.
All inputs are finite; a program needn't handle non-finite values.
Results may differ from a plain program's by a relative error of at most 0.018.
Values may be sent and summed in bfloat16 or wider, within the bound.
A program may use at most 192 MiB of HBM per device.

v0:
```python
import math
import jax
import jax.numpy as jnp
from jax import lax
from jax.sharding import PartitionSpec as P

D = 2048
H = 16
CLIP_TAU = 6
EPSILON = 1e-05
MASKED = -1e30


def rope_tables(length, head_size):
    half_size = head_size // 2
    inverse = 10000.0 ** (-2.0 * jnp.arange(half_size, dtype=jnp.float32) / head_size)
    angles = jnp.arange(length, dtype=jnp.float32)[:, None] * inverse[None, :]
    cosine_table = jnp.cos(angles)
    sine_table = jnp.sin(angles)
    return (
        jnp.concatenate([cosine_table, cosine_table], axis=1),
        jnp.concatenate([sine_table, sine_table], axis=1),
    )


def rotate(values, cosine_table, sine_table):
    half_size = values.shape[-1] // 2
    turned = jnp.concatenate([-values[..., half_size:], values[..., :half_size]], axis=-1)
    return values * cosine_table[:, None, :] + turned * sine_table[:, None, :]


def rotate_back(grads, cosine_table, sine_table):
    half_size = grads.shape[-1] // 2
    scaled = grads * sine_table[:, None, :]
    turned = jnp.concatenate([scaled[..., half_size:], -scaled[..., :half_size]], axis=-1)
    return grads * cosine_table[:, None, :] + turned


def mix_inputs(weights_in, stream_set):
    return jnp.sum(weights_in[:, None, None] * stream_set, axis=0)


def mix_streams(matrix, stream_set):
    return jnp.sum(matrix[:, :, None, None] * stream_set[None, :, :, :], axis=1)


def mix_back(matrix, grads):
    return jnp.sum(matrix[:, :, None, None] * grads[:, None, :, :], axis=0)


def hyper_rows(pre_grad, post_grad, mix_grad):
    return jnp.concatenate([pre_grad[:, None], post_grad[:, None], mix_grad], axis=1)


def span_labels(positions, starts, lengths):
    inside = (positions[:, None] >= starts[None, :]) & (
        positions[:, None] < (starts + lengths)[None, :]
    )
    numbers = jnp.arange(1, starts.shape[0] + 1, dtype=jnp.int32)
    return jnp.sum(jnp.where(inside, numbers[None, :], 0), axis=1)


def block_mask(doc_row, labels, start_row, count_rows):
    key_pos = jnp.arange(doc_row.shape[0], dtype=jnp.int32)
    query_pos = start_row + jnp.arange(count_rows, dtype=jnp.int32)
    query_docs = lax.dynamic_slice_in_dim(doc_row, start_row, count_rows)
    query_labels = lax.dynamic_slice_in_dim(labels, start_row, count_rows)
    same_doc = query_docs[:, None] == doc_row[None, :]
    causal = key_pos[None, :] <= query_pos[:, None]
    joint_span = (query_labels[:, None] > 0) & (query_labels[:, None] == labels[None, :])
    return same_doc & (causal | joint_span)


def attend_forward(queries, keys_roped, values, doc_row, starts, lengths, score_scale):
    length, head_count, head_size = queries.shape
    block_rows = min(512, length)
    labels = span_labels(jnp.arange(length, dtype=jnp.int32), starts, lengths)

    def one_block(block_index):
        start_row = block_index * block_rows
        query_rows = lax.dynamic_slice_in_dim(queries, start_row, block_rows, 0)
        scores = (
            jnp.einsum("qhd,khd->hqk", query_rows, keys_roped, preferred_element_type=jnp.float32)
            * score_scale
        )
        allowed = block_mask(doc_row, labels, start_row, block_rows)
        masked = jnp.where(allowed[None, :, :], scores, MASKED)
        largest = jnp.max(masked, axis=2)
        exponent = jnp.exp(masked - largest[:, :, None])
        totals = jnp.sum(exponent, axis=2)
        weights_low = (exponent / totals[:, :, None]).astype(jnp.bfloat16)
        attended = jnp.einsum(
            "hqk,khd->qhd", weights_low, values, preferred_element_type=jnp.float32
        )
        return (attended, largest + jnp.log(totals), jnp.max(largest, axis=1))

    attended, log_sums, block_tops = lax.map(
        one_block, jnp.arange(length // block_rows, dtype=jnp.int32)
    )
    return (attended.reshape(length, head_count, head_size), log_sums, jnp.max(block_tops, axis=0))


def attend_backward(
    queries, keys_roped, values, dout, log_sums, doc_row, starts, lengths, score_scale
):
    length, head_count, head_size = queries.shape
    block_rows = min(512, length)
    labels = span_labels(jnp.arange(length, dtype=jnp.int32), starts, lengths)

    def one_block(carry, inputs):
        key_grad, value_grad = carry
        block_index, log_rows = inputs
        start_row = block_index * block_rows
        query_rows = lax.dynamic_slice_in_dim(queries, start_row, block_rows, 0)
        dout_rows = lax.dynamic_slice_in_dim(dout, start_row, block_rows, 0)
        scores = (
            jnp.einsum("qhd,khd->hqk", query_rows, keys_roped, preferred_element_type=jnp.float32)
            * score_scale
        )
        allowed = block_mask(doc_row, labels, start_row, block_rows)
        masked = jnp.where(allowed[None, :, :], scores, MASKED)
        weights_full = jnp.where(allowed[None, :, :], jnp.exp(masked - log_rows[:, :, None]), 0.0)
        weight_grad = jnp.einsum(
            "qhd,khd->hqk", dout_rows, values, preferred_element_type=jnp.float32
        )
        centre = jnp.sum(weights_full * weight_grad, axis=2, keepdims=True)
        score_grad = (weights_full * (weight_grad - centre)).astype(jnp.bfloat16)
        query_grad = score_scale * jnp.einsum(
            "hqk,khd->qhd", score_grad, keys_roped, preferred_element_type=jnp.float32
        )
        key_grad = key_grad + score_scale * jnp.einsum(
            "hqk,qhd->khd", score_grad, query_rows, preferred_element_type=jnp.float32
        )
        value_grad = value_grad + jnp.einsum(
            "hqk,qhd->khd",
            weights_full.astype(jnp.bfloat16),
            dout_rows,
            preferred_element_type=jnp.float32,
        )
        return ((key_grad, value_grad), query_grad)

    empty_grad = jnp.zeros((length, head_count, head_size), jnp.float32)
    count_blocks = length // block_rows
    (key_grad, value_grad), query_grad = lax.scan(
        one_block, (empty_grad, empty_grad), (jnp.arange(count_blocks, dtype=jnp.int32), log_sums)
    )
    return (query_grad.reshape(length, head_count, head_size), key_grad, value_grad)


def row_sums(first_term, second_term):
    return lax.psum((jnp.sum(first_term, axis=1), jnp.sum(second_term, axis=1)), "wide")


def features(piece):
    return lax.all_gather(piece, "wide", axis=1, tiled=True)


def branch_rows(partial_value):
    return lax.psum_scatter(partial_value, "wide", scatter_dimension=1, tiled=True)


def norm_forward(hidden):
    local_width = hidden.shape[1]
    full_width = local_width * lax.axis_size("wide")
    row_total, squares = row_sums(hidden, hidden * hidden)
    centre = row_total / full_width
    spread = squares / full_width - centre * centre
    inverse = lax.rsqrt(spread + EPSILON)
    normed = (hidden - centre[:, None]) * inverse[:, None]
    return (features(normed.astype(jnp.bfloat16)), normed, inverse)


def norm_backward(partial_value, normed, inverse):
    full_width = partial_value.shape[1]
    grad_rows = lax.psum_scatter(partial_value, "wide", scatter_dimension=1, tiled=True)
    row_total, row_cross = row_sums(grad_rows, grad_rows * normed)
    return inverse[:, None] * (
        grad_rows - row_total[:, None] / full_width - normed * row_cross[:, None] / full_width
    )


def per_device(
    streams,
    cotangent,
    w_query,
    w_key,
    w_value,
    w_out,
    w_gate,
    w_up,
    w_down,
    hyper,
    doc_ids,
    span_starts,
    span_lengths,
):
    seq_count, length = doc_ids.shape
    tokens = streams.shape[1]
    head_size = D // H
    column_count = w_query.shape[1]
    head_count = column_count // head_size
    score_scale = 1.0 / math.sqrt(head_size)
    cosine_table, sine_table = rope_tables(length, head_size)
    shape_heads = (seq_count, length, head_count, head_size)
    attn_pre, attn_post, attn_mix = (hyper[0, :, 0], hyper[0, :, 1], hyper[0, :, 2:])
    ffn_pre, ffn_post, ffn_mix = (hyper[1, :, 0], hyper[1, :, 1], hyper[1, :, 2:])
    query_w, key_w, value_w, out_w = (
        lax.all_gather(w_query, "dp", axis=0, tiled=True),
        lax.all_gather(w_key, "dp", axis=0, tiled=True),
        lax.all_gather(w_value, "dp", axis=0, tiled=True),
        lax.all_gather(w_out, "dp", axis=1, tiled=True),
    )
    gate_w, up_w, down_w = (
        lax.all_gather(w_gate, "dp", axis=0, tiled=True),
        lax.all_gather(w_up, "dp", axis=0, tiled=True),
        lax.all_gather(w_down, "dp", axis=1, tiled=True),
    )
    normed_one, kept_one, inverse_one = norm_forward(mix_inputs(attn_pre, streams))
    query_raw = jnp.dot(normed_one, query_w, preferred_element_type=jnp.float32).reshape(
        shape_heads
    )
    key_raw = jnp.dot(normed_one, key_w, preferred_element_type=jnp.float32).reshape(shape_heads)
    values = (
        jnp.dot(normed_one, value_w, preferred_element_type=jnp.float32)
        .astype(jnp.bfloat16)
        .reshape(shape_heads)
    )
    queries = rotate(query_raw, cosine_table, sine_table).astype(jnp.bfloat16)
    keys_roped = rotate(key_raw, cosine_table, sine_table).astype(jnp.bfloat16)

    def forward_sequence(inputs):
        return attend_forward(
            inputs[0], inputs[1], inputs[2], inputs[3], inputs[4], inputs[5], score_scale
        )

    attended, log_sums, seq_tops = lax.map(
        forward_sequence, (queries, keys_roped, values, doc_ids, span_starts, span_lengths)
    )
    head_top = lax.pmax(jnp.max(seq_tops, axis=0), "dp")
    attended_low = attended.reshape(tokens, column_count).astype(jnp.bfloat16)
    branch_one = branch_rows(jnp.dot(attended_low, out_w, preferred_element_type=jnp.float32))
    after_attn = mix_streams(attn_mix, streams) + attn_post[:, None, None] * branch_one[None, :, :]
    normed_two, kept_two, inverse_two = norm_forward(mix_inputs(ffn_pre, after_attn))
    gate_proj = jnp.dot(normed_two, gate_w, preferred_element_type=jnp.float32)
    up_proj = jnp.dot(normed_two, up_w, preferred_element_type=jnp.float32)
    sigmoid_gate = jax.nn.sigmoid(gate_proj)
    hidden = (gate_proj * sigmoid_gate * up_proj).astype(jnp.bfloat16)
    branch_two = branch_rows(jnp.dot(hidden, down_w, preferred_element_type=jnp.float32))
    out_streams = (
        mix_streams(ffn_mix, after_attn) + ffn_post[:, None, None] * branch_two[None, :, :]
    )
    ffn_post_grad = jnp.sum(cotangent * branch_two[None, :, :], axis=(1, 2))
    ffn_mix_grad = jnp.sum(cotangent[:, None, :, :] * after_attn[None, :, :, :], axis=(2, 3))
    two_grad = features(jnp.sum(ffn_post[:, None, None] * cotangent, axis=0).astype(jnp.bfloat16))
    hidden_grad = jnp.dot(two_grad, down_w.T, preferred_element_type=jnp.float32)
    down_wgrad = jnp.einsum("tf,td->fd", hidden, two_grad, preferred_element_type=jnp.float32)
    gate_grad = (
        hidden_grad * up_proj * sigmoid_gate * (1.0 + gate_proj * (1.0 - sigmoid_gate))
    ).astype(jnp.bfloat16)
    up_grad = (hidden_grad * gate_proj * sigmoid_gate).astype(jnp.bfloat16)
    gate_wgrad = jnp.einsum("td,tf->df", normed_two, gate_grad, preferred_element_type=jnp.float32)
    up_wgrad = jnp.einsum("td,tf->df", normed_two, up_grad, preferred_element_type=jnp.float32)
    gate_shard, up_shard, down_shard = (
        lax.psum_scatter(gate_wgrad, "dp", scatter_dimension=0, tiled=True),
        lax.psum_scatter(up_wgrad, "dp", scatter_dimension=0, tiled=True),
        lax.psum_scatter(down_wgrad, "dp", scatter_dimension=1, tiled=True),
    )
    normed_two_grad = jnp.dot(gate_grad, gate_w.T, preferred_element_type=jnp.float32) + jnp.dot(
        up_grad, up_w.T, preferred_element_type=jnp.float32
    )
    h_two_grad = norm_backward(normed_two_grad, kept_two, inverse_two)
    ffn_pre_grad = jnp.sum(h_two_grad[None, :, :] * after_attn, axis=(1, 2))
    after_grad = mix_back(ffn_mix, cotangent) + ffn_pre[:, None, None] * h_two_grad[None, :, :]
    attn_post_grad = jnp.sum(after_grad * branch_one[None, :, :], axis=(1, 2))
    attn_mix_grad = jnp.sum(after_grad[:, None, :, :] * streams[None, :, :, :], axis=(2, 3))
    one_grad = features(jnp.sum(attn_post[:, None, None] * after_grad, axis=0).astype(jnp.bfloat16))
    attended_grad = jnp.dot(one_grad, out_w.T, preferred_element_type=jnp.float32).astype(
        jnp.bfloat16
    )
    out_wgrad = jnp.einsum("tc,td->cd", attended_low, one_grad, preferred_element_type=jnp.float32)

    def backward_sequence(inputs):
        return attend_backward(
            inputs[0],
            inputs[1],
            inputs[2],
            inputs[3],
            inputs[4],
            inputs[5],
            inputs[6],
            inputs[7],
            score_scale,
        )

    query_grad, key_grad, value_grad = lax.map(
        backward_sequence,
        (
            queries,
            keys_roped,
            values,
            attended_grad.reshape(shape_heads),
            log_sums,
            doc_ids,
            span_starts,
            span_lengths,
        ),
    )
    query_low = (
        rotate_back(query_grad, cosine_table, sine_table)
        .reshape(tokens, column_count)
        .astype(jnp.bfloat16)
    )
    key_low = (
        rotate_back(key_grad, cosine_table, sine_table)
        .reshape(tokens, column_count)
        .astype(jnp.bfloat16)
    )
    value_low = value_grad.reshape(tokens, column_count).astype(jnp.bfloat16)
    query_wgrad = jnp.einsum("td,tc->dc", normed_one, query_low, preferred_element_type=jnp.float32)
    key_wgrad = jnp.einsum("td,tc->dc", normed_one, key_low, preferred_element_type=jnp.float32)
    value_wgrad = jnp.einsum("td,tc->dc", normed_one, value_low, preferred_element_type=jnp.float32)
    normed_one_grad = (
        jnp.dot(query_low, query_w.T, preferred_element_type=jnp.float32)
        + jnp.dot(key_low, key_w.T, preferred_element_type=jnp.float32)
        + jnp.dot(value_low, value_w.T, preferred_element_type=jnp.float32)
    )
    h_one_grad = norm_backward(normed_one_grad, kept_one, inverse_one)
    attn_pre_grad = jnp.sum(h_one_grad[None, :, :] * streams, axis=(1, 2))
    streams_grad = mix_back(attn_mix, after_grad) + attn_pre[:, None, None] * h_one_grad[None, :, :]
    hyper_grad = lax.psum(
        jnp.stack(
            [
                hyper_rows(attn_pre_grad, attn_post_grad, attn_mix_grad),
                hyper_rows(ffn_pre_grad, ffn_post_grad, ffn_mix_grad),
            ]
        ),
        ("dp", "wide"),
    )
    query_shard, key_shard, value_shard, out_shard = (
        lax.psum_scatter(query_wgrad, "dp", scatter_dimension=0, tiled=True),
        lax.psum_scatter(key_wgrad, "dp", scatter_dimension=0, tiled=True),
        lax.psum_scatter(value_wgrad, "dp", scatter_dimension=0, tiled=True),
        lax.psum_scatter(out_wgrad, "dp", scatter_dimension=1, tiled=True),
    )
    clip_scale = jnp.sqrt(CLIP_TAU / jnp.maximum(head_top, CLIP_TAU))
    columns = jnp.repeat(clip_scale, head_size)[None, :]
    return (
        out_streams,
        streams_grad,
        query_shard,
        key_shard,
        value_shard,
        out_shard,
        gate_shard,
        up_shard,
        down_shard,
        hyper_grad,
        clip_scale,
        w_query.astype(jnp.float32) * columns,
        w_key.astype(jnp.float32) * columns,
    )


def solution(mesh):
    return jax.shard_map(
        per_device,
        mesh=mesh,
        in_specs=(
            P(None, "dp", "wide"),
            P(None, "dp", "wide"),
            P("dp", "wide"),
            P("dp", "wide"),
            P("dp", "wide"),
            P("wide", "dp"),
            P("dp", "wide"),
            P("dp", "wide"),
            P("wide", "dp"),
            P(),
            P("dp", None),
            P("dp", None),
            P("dp", None),
        ),
        out_specs=(
            P(None, "dp", "wide"),
            P(None, "dp", "wide"),
            P("dp", "wide"),
            P("dp", "wide"),
            P("dp", "wide"),
            P("wide", "dp"),
            P("dp", "wide"),
            P("dp", "wide"),
            P("wide", "dp"),
            P(),
            P("wide"),
            P("dp", "wide"),
            P("dp", "wide"),
        ),
        check_vma=False,
    )
```

profile of v0, /device:TPU:0, one launch (start us, length us, event | category | flops | bytes accessed | tf_op | source)
XLA Modules:
  0.0 1579.7 jit_solution(8456090871075567823)
XLA Ops:
  11.9 23.4 %all-reduce.3 = (f32[1024]{0:T(1024)S(1)}, f32[1024]{0:T(1024)S(1)}) all-reduce(f32[1024]{0:T(1024)S(1)} %multiply_reduce_fusion.20, f32[1024]{0:T(1024)S(1)} %get-tuple-element.312), channel_id=1, replica_groups=mesh['dp'=4,'wide'=8] {'wide'}, use_global_device_ids=true, to_apply=%region_5.6 | all-reduce | flops 2048 | bytes 16384 | tf_op jit(solution)/shard_map/psum | solution.py:151
  42.8 66.4 %all-gather.12.cloned.1.call-done = bf16[1024,2048]{1,0:T(8,128)(2,1)} async-done(((bf16[1024,256]{1,0:T(8,128)(2,1)}), bf16[1024,2048]{1,0:T(8,128)(2,1)}) %all-gather.12.cloned.1.call-update) | async-done | bytes 4194320 | tf_op jit(solution)/shard_map/all_gather | solution.py:155
  147.9 14.2 while.53
  175.5 141.2 %reduce-scatter.12.cloned.1.call-done = f32[1024,256]{1,0:T(8,128)} async-done(((f32[1024,2048]{1,0:T(8,128)}), f32[1024,256]{1,0:T(8,128)}) %reduce-scatter.12.cloned.1.call-update) | async-done | bytes 1048592 | tf_op jit(solution)/shard_map/reduce_scatter | solution.py:159
  322.2 19.7 %all-reduce.2 = (f32[1024]{0:T(1024)S(1)}, f32[1024]{0:T(1024)S(1)}) all-reduce(f32[1024]{0:T(1024)S(1)} %multiply_reduce_fusion.19, f32[1024]{0:T(1024)S(1)} %get-tuple-element.310), channel_id=1, replica_groups=mesh['dp'=4,'wide'=8] {'wide'}, use_global_device_ids=true, to_apply=%region_18.19 | all-reduce | flops 2048 | bytes 16384 | tf_op jit(solution)/shard_map/psum | solution.py:151
  351.8 77.3 %all-gather.22.cloned.1.call-done = bf16[1024,2048]{1,0:T(8,128)(2,1)} async-done(((bf16[1024,256]{1,0:T(8,128)(2,1)}), bf16[1024,2048]{1,0:T(8,128)(2,1)}) %all-gather.22.cloned.1.call-update) | async-done | bytes 4194320 | tf_op jit(solution)/shard_map/all_gather | solution.py:155
  439.1 24.3 %all-gather.26.cloned.1.call-done = bf16[2048,1024]{1,0:T(8,128)(2,1)} async-done(((bf16[512,1024]{1,0:T(8,128)(2,1)}), bf16[2048,1024]{1,0:T(8,128)(2,1)}) %all-gather.26.cloned.1.call-update) | async-done | bytes 4194320 | tf_op jit(solution)/shard_map/all_gather | solution.py:215
  475.4 23.8 %all-gather.28.cloned.1.call-done = bf16[1024,2048]{1,0:T(8,128)(2,1)} async-done(((bf16[1024,512]{1,0:T(8,128)(2,1)}), bf16[1024,2048]{1,0:T(8,128)(2,1)}) %all-gather.28.cloned.1.call-update) | async-done | bytes 4194320 | tf_op jit(solution)/shard_map/all_gather | solution.py:216
  520.7 137.2 %reduce-scatter.14.cloned.1.call-done = f32[1024,256]{1,0:T(8,128)} async-done(((f32[1024,2048]{1,0:T(8,128)}), f32[1024,256]{1,0:T(8,128)}) %reduce-scatter.14.cloned.1.call-update) | async-done | bytes 1048592 | tf_op jit(solution)/shard_map/reduce_scatter | solution.py:159
  666.3 73.4 %all-gather.30.cloned.1.call-done = bf16[1024,2048]{1,0:T(8,128)(2,1)} async-done(((bf16[1024,256]{1,0:T(8,128)(2,1)}), bf16[1024,2048]{1,0:T(8,128)(2,1)}) %all-gather.30.cloned.1.call-update) | async-done | bytes 4194320 | tf_op jit(solution)/shard_map/all_gather | solution.py:155
  739.7 12.9 multiply_convert_fusion.1
  766.6 146.1 %reduce-scatter.16.cloned.1.call-done = f32[1024,256]{1,0:T(8,128)} async-done(((f32[1024,2048]{1,0:T(8,128)}), f32[1024,256]{1,0:T(8,128)}) %reduce-scatter.16.cloned.1.call-update) | async-done | bytes 1048592 | tf_op jit(solution)/shard_map/reduce_scatter | solution.py:175
  914.6 19.9 %all-reduce.1 = (f32[1024]{0:T(1024)S(1)}, f32[1024]{0:T(1024)S(1)}) all-reduce(f32[1024]{0:T(1024)S(1)} %get-tuple-element.326, f32[1024]{0:T(1024)S(1)} %get-tuple-element.325), channel_id=1, replica_groups=mesh['dp'=4,'wide'=8] {'wide'}, use_global_device_ids=true, to_apply=%region_26.27 | all-reduce | flops 2048 | bytes 16384 | tf_op jit(solution)/shard_map/psum | solution.py:151
  948.7 68.3 %all-gather.32.cloned.1.call-done = bf16[1024,2048]{1,0:T(8,128)(2,1)} async-done(((bf16[1024,256]{1,0:T(8,128)(2,1)}), bf16[1024,2048]{1,0:T(8,128)(2,1)}) %all-gather.32.cloned.1.call-update) | async-done | bytes 4194320 | tf_op jit(solution)/shard_map/all_gather | solution.py:155
  1020.7 30.5 %while.54 = (s32[]{:T(128)}, f32[1024,2,128]{0,2,1:T(8,128)S(1)}, f32[1024,2,128]{0,2,1:T(8,128)}, f32[2,512,2,128]{3,1,2,0:T(8,128)}, s32[2]{0:T(128)S(1)}, /*i...) while((s32[]{:T(128)}, f32[1024,2,128]{0,2,1:T(8,128)S(1)}, ...), condition=%wide.region_31.32_spmd.clone.clone, body=%wide.region_29.31_spmd.clone.sunk.clone | while | flops 1357250560 | bytes 90224648 | solution.py:144
  1135.9 76.0 %reduce-scatter.18.cloned.1.call-done = f32[1024,256]{1,0:T(8,128)} async-done(((f32[1024,2048]{1,0:T(8,128)}), f32[1024,256]{1,0:T(8,128)}) %reduce-scatter.18.cloned.1.call-update) | async-done | bytes 1048592 | tf_op jit(solution)/shard_map/reduce_scatter | solution.py:175
  1213.8 19.7 %all-reduce = (f32[1024]{0:T(1024)S(1)}, f32[1024]{0:T(1024)S(1)}) all-reduce(f32[1024]{0:T(1024)S(1)} %get-tuple-element.324, f32[1024]{0:T(1024)S(1)} %get-tuple-element.323), channel_id=1, replica_groups=mesh['dp'=4,'wide'=8] {'wide'}, use_global_device_ids=true, to_apply=%region_36.37 | all-reduce | flops 2048 | bytes 16384 | tf_op jit(solution)/shard_map/psum | solution.py:151
  1242.9 38.0 %psum.71 = f32[2,4,6]{2,1,0:T(4,128)} all-reduce(f32[2,4,6]{2,1,0:T(4,128)S(1)} %pad_maximum_fusion.3), channel_id=1, replica_groups=mesh['dp'=4,'wide'=8] {'dp','wide'}, use_global_device_ids=true, to_apply=%region_50.51 | all-reduce | flops 48 | bytes 384 | tf_op jit(solution)/shard_map/psum | solution.py:330
  1286.7 74.4 %reduce-scatter.28.cloned.1.call-done = f32[512,1024]{1,0:T(8,128)} async-done(((f32[2048,1024]{1,0:T(8,128)}), f32[512,1024]{1,0:T(8,128)}) %reduce-scatter.28.cloned.1.call-update) | async-done | bytes 2097168 | tf_op jit(solution)/shard_map/reduce_scatter | solution.py:264
  1361.1 74.4 %reduce-scatter.30.cloned.1.call-done = f32[512,1024]{1,0:T(8,128)} async-done(((f32[2048,1024]{1,0:T(8,128)}), f32[512,1024]{1,0:T(8,128)}) %reduce-scatter.30.cloned.1.call-update) | async-done | bytes 2097168 | tf_op jit(solution)/shard_map/reduce_scatter | solution.py:265
  1435.6 34.3 %reduce-scatter.22.cloned.1.call-done = f32[512,256]{1,0:T(8,128)} async-done(((f32[2048,256]{1,0:T(8,128)}), f32[512,256]{1,0:T(8,128)}) %reduce-scatter.22.cloned.1.call-update) | async-done | bytes 524304 | tf_op jit(solution)/shard_map/reduce_scatter | solution.py:341
  1469.9 34.2 %reduce-scatter.20.cloned.1.call-done = f32[512,256]{1,0:T(8,128)} async-done(((f32[2048,256]{1,0:T(8,128)}), f32[512,256]{1,0:T(8,128)}) %reduce-scatter.20.cloned.1.call-update) | async-done | bytes 524304 | tf_op jit(solution)/shard_map/reduce_scatter | solution.py:340
  1504.0 34.3 %reduce-scatter.26.cloned.1.call-done = f32[256,512]{1,0:T(8,128)} async-done(((f32[256,2048]{1,0:T(8,128)}), f32[256,512]{1,0:T(8,128)}) %reduce-scatter.26.cloned.1.call-update) | async-done | bytes 524304 | tf_op jit(solution)/shard_map/reduce_scatter | solution.py:343
  1538.4 34.3 %reduce-scatter.24.cloned.1.call-done = f32[512,256]{1,0:T(8,128)} async-done(((f32[2048,256]{1,0:T(8,128)}), f32[512,256]{1,0:T(8,128)}) %reduce-scatter.24.cloned.1.call-update) | async-done | bytes 524304 | tf_op jit(solution)/shard_map/reduce_scatter | solution.py:342
  (302 shorter events, 307.1 us)
Async XLA Ops:
  7.2 35.6 %all-gather.16.cloned.1.call-start = ((), (), s32[]{:S(2)}) async-start(), calls=%async_computation.13 | async-start | bytes 1310720 | tf_op jit(solution)/shard_map/all_gather | solution.py:209
  7.9 101.3 %all-gather.12.cloned.1.call-start = ((), (), s32[]{:S(2)}) async-start(), calls=%async_computation.11 | async-start | bytes 4718592 | tf_op jit(solution)/shard_map/all_gather | solution.py:155
  37.1 88.5 %all-gather.14.cloned.1.call-start = ((), (), s32[]{:S(2)}) async-start(), calls=%async_computation.12 | async-start | bytes 1310720 | tf_op jit(solution)/shard_map/all_gather | solution.py:208
  37.9 105.9 %all-gather.18.cloned.1.call-start = ((), (), s32[]{:S(2)}) async-start(), calls=%async_computation.14 | async-start | bytes 1310720 | tf_op jit(solution)/shard_map/all_gather | solution.py:210
  38.5 124.3 %all-gather.20.cloned.1.call-start = ((), (), s32[]{:S(2)}) async-start(), calls=%async_computation.15 | async-start | bytes 1310720 | tf_op jit(solution)/shard_map/all_gather | solution.py:211
  39.0 277.6 %reduce-scatter.12.cloned.1.call-start = ((), (), s32[]{:S(2)}) async-start(), calls=%async_computation.16 | async-start | bytes 9437184 | tf_op jit(solution)/shard_map/reduce_scatter | solution.py:159
  42.5 902.6 %copy-start.12 = (f32[1024,128]{0,1:T(8,128)}, f32[1024,128]{0,1:T(8,128)S(1)}, u32[]{:S(2)}) copy-start(f32[1024,128]{0,1:T(8,128)S(1)} %copy.61) | copy-start | bytes 1572868
  168.6 183.2 %all-gather.24.cloned.1.call-start = ((), (), s32[]{:S(2)}) async-start(), calls=%async_computation.18 | async-start | bytes 5242880 | tf_op jit(solution)/shard_map/all_gather | solution.py:214
  169.4 259.7 %all-gather.22.cloned.1.call-start = ((), (), s32[]{:S(2)}) async-start(), calls=%async_computation.17 | async-start | bytes 4718592 | tf_op jit(solution)/shard_map/all_gather | solution.py:155
  343.1 120.2 %all-gather.26.cloned.1.call-start = ((), (), s32[]{:S(2)}) async-start(), calls=%async_computation.19 | async-start | bytes 5242880 | tf_op jit(solution)/shard_map/all_gather | solution.py:215
  343.8 155.4 %all-gather.28.cloned.1.call-start = ((), (), s32[]{:S(2)}) async-start(), calls=%async_computation.20 | async-start | bytes 5242880 | tf_op jit(solution)/shard_map/all_gather | solution.py:216
  344.4 313.4 %reduce-scatter.14.cloned.1.call-start = ((), (), s32[]{:S(2)}) async-start(), calls=%async_computation.21 | async-start | bytes 9437184 | tf_op jit(solution)/shard_map/reduce_scatter | solution.py:159
  509.8 229.9 %all-gather.30.cloned.1.call-start = ((), (), s32[]{:S(2)}) async-start(), calls=%async_computation.22 | async-start | bytes 4718592 | tf_op jit(solution)/shard_map/all_gather | solution.py:155
  665.9 246.9 %reduce-scatter.16.cloned.1.call-start = ((), (), s32[]{:S(2)}) async-start(), calls=%async_computation.23 | async-start | bytes 9437184 | tf_op jit(solution)/shard_map/reduce_scatter | solution.py:175
  766.6 250.4 %all-gather.32.cloned.1.call-start = ((), (), s32[]{:S(2)}) async-start(), calls=%async_computation.24 | async-start | bytes 4718592 | tf_op jit(solution)/shard_map/all_gather | solution.py:155
  944.9 267.0 %reduce-scatter.18.cloned.1.call-start = ((), (), s32[]{:S(2)}) async-start(), calls=%async_computation.25 | async-start | bytes 9437184 | tf_op jit(solution)/shard_map/reduce_scatter | solution.py:175
  1065.7 221.0 %reduce-scatter.32.cloned.1.call-start = ((), (), s32[]{:S(2)}) async-start(), calls=%async_computation.32 | async-start | bytes 10485760 | tf_op jit(solution)/shard_map/reduce_scatter | solution.py:266
  1076.6 284.5 %reduce-scatter.28.cloned.1.call-start = ((), (), s32[]{:S(2)}) async-start(), calls=%async_computation.30 | async-start | bytes 10485760 | tf_op jit(solution)/shard_map/reduce_scatter | solution.py:264
  1087.4 348.2 %reduce-scatter.30.cloned.1.call-start = ((), (), s32[]{:S(2)}) async-start(), calls=%async_computation.31 | async-start | bytes 10485760 | tf_op jit(solution)/shard_map/reduce_scatter | solution.py:265
  1098.6 371.3 %reduce-scatter.22.cloned.1.call-start = ((), (), s32[]{:S(2)}) async-start(), calls=%async_computation.27 | async-start | bytes 2621440 | tf_op jit(solution)/shard_map/reduce_scatter | solution.py:341
  1103.5 400.5 %reduce-scatter.20.cloned.1.call-start = ((), (), s32[]{:S(2)}) async-start(), calls=%async_computation.26 | async-start | bytes 2621440 | tf_op jit(solution)/shard_map/reduce_scatter | solution.py:340
  1108.6 429.7 %reduce-scatter.26.cloned.1.call-start = ((), (), s32[]{:S(2)}) async-start(), calls=%async_computation.29 | async-start | bytes 2621440 | tf_op jit(solution)/shard_map/reduce_scatter | solution.py:343
  1113.9 458.8 %reduce-scatter.24.cloned.1.call-start = ((), (), s32[]{:S(2)}) async-start(), calls=%async_computation.28 | async-start | bytes 2621440 | tf_op jit(solution)/shard_map/reduce_scatter | solution.py:342
  1135.9 99.5 %copy-start.39 = (f32[4]{0:T(128)S(1)}, f32[4]{0:T(128)}, u32[]{:S(2)}) copy-start(f32[4]{0:T(128)} %copy-done.38) | copy-start | bytes 52
  (57 other events, 722.8 us)
Sparse Core Ops, SparseCore 0:
  9.5 19.4 all-gather.15
  37.3 71.8 all-gather.11
  110.8 14.8 all-gather.13
  127.1 16.6 all-gather.17
  145.2 16.6 all-gather.19
  168.7 147.8 reduce-scatter.11
  318.2 33.5 all-gather.23
  354.4 74.6 all-gather.21
  430.7 32.6 all-gather.25
  464.7 34.4 all-gather.27
  509.9 147.8 reduce-scatter.13
  666.0 73.7 all-gather.29
  766.7 146.0 reduce-scatter.15
  945.1 71.8 all-gather.31
  1065.9 146.0 reduce-scatter.17
  1214.9 71.7 reduce-scatter.31
  1289.7 71.3 reduce-scatter.27
  1364.1 71.3 reduce-scatter.29
  1438.7 31.1 reduce-scatter.21
  1472.8 31.1 reduce-scatter.19
  1507.2 31.1 reduce-scatter.25
  1541.5 31.1 reduce-scatter.23
where the time goes:
time: 1590 us; the launch traced here: 1580 us
  waiting for transfers between devices  1160 us (73%)
  matrix products  165 us (10%)
  blocking collectives  127 us (8%)
  other arithmetic  86.2 us (5%)
  local copies, waits for them, and re-layouts  21 us (1%)
    all_gather x4, waiting for transfers between devices, features(): return lax.all_gather(piece, 'wide', axis=1, tiled=True)  285 us
    reduce_scatter x2, waiting for transfers between devices, branch_rows(): lax.psum_scatter(partial_value, 'wide', scatter_dimension=1, tiled=True)  278 us
    reduce_scatter x2, waiting for transfers between devices, norm_backward(): lax.psum_scatter(partial_value, 'wide', scatter_dimension=1, tiled=True)  222 us
    psum x4, blocking collectives, row_sums(): lax.psum((jnp.sum(first_term, axis=1), jnp.sum(second_term, axis=1)), 'wi...  82.8 us
    reduce_scatter x1, waiting for transfers between devices, per_device(): lax.psum_scatter(up_wgrad, 'dp', scatter_dimension=0, tiled=True)  74.4 us
    reduce_scatter x1, waiting for transfers between devices, per_device(): lax.psum_scatter(gate_wgrad, 'dp', scatter_dimension=0, tiled=True)  74.4 us
    psum x1, blocking collectives, per_device(): lax.psum(jnp.stack([hyper_rows(attn_pre_grad, attn_post_grad, attn_mix_gr...  38 us
    reduce_scatter x1, waiting for transfers between devices, per_device(): lax.psum_scatter(out_wgrad, 'dp', scatter_dimension=1, tiled=True)  34.3 us
  transfers between devices with their start and end apart: 22, of which 20 were waited for; matrix products, arithmetic and copies ran while one was open for 10% of the time, Pallas kernels for 0%

commit v1 on v0

--- a/solution.py
+++ b/solution.py
@@ -1,3 +1,4 @@
+import functools
 import math
 import jax
 import jax.numpy as jnp
@@ -9,6 +10,36 @@
 CLIP_TAU = 6
 EPSILON = 1e-05
 MASKED = -1e30
+
+
+def _report_spot(inp, link_axis):
+    moved = lax.axis_size(link_axis)
+    q_next = lax.axis_index(link_axis)
+    carry_out, lower, response = (moved, q_next, inp.shape[1])
+    blocks_here = [ix * carry_out if k == 1 else ix for k, ix in enumerate(inp.shape)]
+    small = jnp.zeros(blocks_here, inp.dtype)
+    latest = lax.dynamic_update_slice_in_dim(small, inp, lower * response, axis=1)
+    built = f_next = inp
+    for to_i in range(1, carry_out // 2 + 1):
+        after = range(carry_out)
+        u_next = map(lambda k: (k, (k + 1) % carry_out), after)
+        e_next = list(u_next)
+        built = lax.ppermute(built, axis_name=link_axis, perm=e_next)
+        latest = lax.dynamic_update_slice_in_dim(
+            latest, built, (lower - to_i) % carry_out * response, axis=1
+        )
+        if 2 * to_i < carry_out:
+            arr_out = range(carry_out)
+            upper = map(lambda k: (k, (k - 1) % carry_out), arr_out)
+            fresh = list(upper)
+            f_next = lax.ppermute(f_next, axis_name=link_axis, perm=fresh)
+            latest = lax.dynamic_update_slice_in_dim(
+                latest, f_next, (lower + to_i) % carry_out * response, axis=1
+            )
+    return latest
+
+
+get_the_ways = functools.partial(_report_spot, link_axis="wide")
 
 
 def rope_tables(length, head_size):
@@ -152,7 +183,7 @@
 
 
 def features(piece):
-    return lax.all_gather(piece, "wide", axis=1, tiled=True)
+    return get_the_ways(piece)
 
 
 def branch_rows(partial_value):

time: 1590 us -> 1540 us (0.969)
  waiting for transfers between devices: 1160 us -> 1020 us
  starting transfers between devices: 2.09 us -> 77.3 us
  local copies, waits for them, and re-layouts: 21 us -> 46.7 us
    all_gather x4 -> x0, waiting for transfers between devices: 285 us -> none  [features(): return lax.all_gather(piece, 'wide', axis=1, tiled=True)]
    ppermute x0 -> x28, waiting for transfers between devices: none -> 233 us  [the longest x16 233 us: _report_spot(): built = lax.ppermute(built, axis_name=link_axis, perm=e_next)]
    ppermute x0 -> x28, starting transfers between devices: none -> 75.6 us  [the longest x12 43.5 us: _report_spot(): f_next = lax.ppermute(f_next, axis_name=link_axis, perm=fresh)]
    all_gather x1, waiting for transfers between devices: 24.3 us -> 0.01 us  [per_device(): lax.all_gather(w_up, 'dp', axis=0, tiled=True)]
    all_gather x1, waiting for transfers between devices: 23.8 us -> 0.01 us  [per_device(): lax.all_gather(w_down, 'dp', axis=1, tiled=True)]
    dynamic_update_slice x0 -> x30, local copies, waits for them, and re-layouts: none -> 19.1 us  [the longest x16 10.4 us: _report_spot(): lax.dynamic_update_slice_in_dim(latest, built, (lower - to_i) % carry_out...]
  transfers between devices with their start and end apart: 22 -> 46, of which waited for: 20 -> 27; matrix products, arithmetic and copies ran while one was open for 10% -> 12% of each run, Pallas kernels for 0% -> 0%
where the time goes in v1:
time: 1540 us; the launch traced here: 1530 us
  waiting for transfers between devices  1020 us (66%)
  matrix products  160 us (10%)
  blocking collectives  127 us (8%)
  other arithmetic  84.9 us (6%)
  starting transfers between devices  77.3 us (5%)
  local copies, waits for them, and re-layouts  46.7 us (3%)
  between operations  15.8 us (1%)
    reduce_scatter x2, waiting for transfers between devices, branch_rows(): lax.psum_scatter(partial_value, 'wide', scatter_dimension=1, tiled=True)  270 us
    ppermute x16, waiting for transfers between devices, _report_spot(): built = lax.ppermute(built, axis_name=link_axis, perm=e_next)  233 us
    reduce_scatter x2, waiting for transfers between devices, norm_backward(): lax.psum_scatter(partial_value, 'wide', scatter_dimension=1, tiled=True)  220 us
    psum x4, blocking collectives, row_sums(): lax.psum((jnp.sum(first_term, axis=1), jnp.sum(second_term, axis=1)), 'wi...  82.6 us
    reduce_scatter x1, waiting for transfers between devices, per_device(): lax.psum_scatter(gate_wgrad, 'dp', scatter_dimension=0, tiled=True)  74.6 us
    reduce_scatter x1, waiting for transfers between devices, per_device(): lax.psum_scatter(up_wgrad, 'dp', scatter_dimension=0, tiled=True)  74.4 us
    ppermute x12, starting transfers between devices, _report_spot(): f_next = lax.ppermute(f_next, axis_name=link_axis, perm=fresh)  43.5 us
    psum x1, blocking collectives, per_device(): lax.psum(jnp.stack([hyper_rows(attn_pre_grad, attn_post_grad, attn_mix_gr...  38 us
  transfers between devices with their start and end apart: 46, of which 27 were waited for; matrix products, arithmetic and copies ran while one was open for 12% of the time, Pallas kernels for 0%

profile of v1, /device:TPU:0, one launch (start us, length us, event | category | flops | bytes accessed | tf_op | source)
XLA Modules:
  0.0 1533.5 jit_solution(16126795838207256441)
XLA Ops:
  13.5 23.4 %all-reduce.3 = (f32[1024]{0:T(1024)S(1)}, f32[1024]{0:T(1024)S(1)}) all-reduce(f32[1024]{0:T(1024)S(1)} %multiply_reduce_fusion.20, f32[1024]{0:T(1024)S(1)} %get-tuple-element.312), channel_id=1, replica_groups=mesh['dp'=4,'wide'=8] {'wide'}, use_global_device_ids=true, to_apply=%region_5.6 | all-reduce | flops 2048 | bytes 16384 | tf_op jit(solution)/shard_map/psum | solution.py:182
  67.8 16.3 %collective-permute-done.2 = bf16[1024,256]{1,0:T(8,128)(2,1)S(1)} collective-permute-done((bf16[1024,256]{1,0:T(8,128)(2,1)S(1)}, bf16[1024,256]{1,0:T(8,128)(2,1)S(1)}, u32[]{:S(2)}, u32[]{:S(2)}) %collective-permute-start.2) | collective-permute-done | bytes 524320 | tf_op jit(solution)/shard_map/ppermute | solution.py:27
  92.0 15.8 %collective-permute-done.4 = bf16[1024,256]{1,0:T(8,128)(2,1)} collective-permute-done((bf16[1024,256]{1,0:T(8,128)(2,1)S(1)}, bf16[1024,256]{1,0:T(8,128)(2,1)}, u32[]{:S(2)}, u32[]{:S(2)}) %collective-permute-start.4) | collective-permute-done | bytes 524320 | tf_op jit(solution)/shard_map/ppermute | solution.py:27
  167.0 136.1 %reduce-scatter.12.cloned.1.call-done = f32[1024,256]{1,0:T(8,128)} async-done(((f32[1024,2048]{1,0:T(8,128)}), f32[1024,256]{1,0:T(8,128)}) %reduce-scatter.12.cloned.1.call-update) | async-done | bytes 1048592 | tf_op jit(solution)/shard_map/reduce_scatter | solution.py:190
  308.6 19.7 %all-reduce.2 = (f32[1024]{0:T(1024)S(1)}, f32[1024]{0:T(1024)S(1)}) all-reduce(f32[1024]{0:T(1024)S(1)} %multiply_reduce_fusion.19, f32[1024]{0:T(1024)S(1)} %get-tuple-element.310), channel_id=1, replica_groups=mesh['dp'=4,'wide'=8] {'wide'}, use_global_device_ids=true, to_apply=%region_18.19 | all-reduce | flops 2048 | bytes 16384 | tf_op jit(solution)/shard_map/psum | solution.py:182
  358.2 17.3 %collective-permute-done.9 = bf16[1024,256]{1,0:T(8,128)(2,1)S(1)} collective-permute-done((bf16[1024,256]{1,0:T(8,128)(2,1)S(1)}, bf16[1024,256]{1,0:T(8,128)(2,1)S(1)}, u32[]{:S(2)}, u32[]{:S(2)}) %collective-permute-start.9) | collective-permute-done | bytes 524320 | tf_op jit(solution)/shard_map/ppermute | solution.py:27
  382.3 17.3 %collective-permute-done.11 = bf16[1024,256]{1,0:T(8,128)(2,1)S(1)} collective-permute-done((bf16[1024,256]{1,0:T(8,128)(2,1)S(1)}, bf16[1024,256]{1,0:T(8,128)(2,1)S(1)}, u32[]{:S(2)}, u32[]{:S(2)}) %collective-permute-start.11) | collective-permute-done | bytes 524320 | tf_op jit(solution)/shard_map/ppermute | solution.py:27
  460.4 133.6 %reduce-scatter.14.cloned.1.call-done = f32[1024,256]{1,0:T(8,128)} async-done(((f32[1024,2048]{1,0:T(8,128)}), f32[1024,256]{1,0:T(8,128)}) %reduce-scatter.14.cloned.1.call-update) | async-done | bytes 1048592 | tf_op jit(solution)/shard_map/reduce_scatter | solution.py:190
  606.3 18.9 %collective-permute-done.14 = bf16[1024,256]{1,0:T(8,128)(2,1)S(1)} collective-permute-done((bf16[1024,256]{1,0:T(8,128)(2,1)S(1)}, bf16[1024,256]{1,0:T(8,128)(2,1)S(1)}, u32[]{:S(2)}, u32[]{:S(2)}) %collective-permute-start.14) | collective-permute-done | bytes 524320 | tf_op jit(solution)/shard_map/ppermute | solution.py:27
  629.9 19.4 %collective-permute-done.16 = bf16[1024,256]{1,0:T(8,128)(2,1)S(1)} collective-permute-done((bf16[1024,256]{1,0:T(8,128)(2,1)S(1)}, bf16[1024,256]{1,0:T(8,128)(2,1)S(1)}, u32[]{:S(2)}, u32[]{:S(2)}) %collective-permute-start.16) | collective-permute-done | bytes 524320 | tf_op jit(solution)/shard_map/ppermute | solution.py:27
  654.7 18.7 %collective-permute-done.18 = bf16[1024,256]{1,0:T(8,128)(2,1)S(1)} collective-permute-done((bf16[1024,256]{1,0:T(8,128)(2,1)S(1)}, bf16[1024,256]{1,0:T(8,128)(2,1)S(1)}, u32[]{:S(2)}, u32[]{:S(2)}) %collective-permute-start.18) | collective-permute-done | bytes 524320 | tf_op jit(solution)/shard_map/ppermute | solution.py:27
  712.6 145.4 %reduce-scatter.16.cloned.1.call-done = f32[1024,256]{1,0:T(8,128)} async-done(((f32[1024,2048]{1,0:T(8,128)}), f32[1024,256]{1,0:T(8,128)}) %reduce-scatter.16.cloned.1.call-update) | async-done | bytes 1048592 | tf_op jit(solution)/shard_map/reduce_scatter | solution.py:206
  859.9 19.7 %all-reduce.1 = (f32[1024]{0:T(1024)S(1)}, f32[1024]{0:T(1024)S(1)}) all-reduce(f32[1024]{0:T(1024)S(1)} %get-tuple-element.326, f32[1024]{0:T(1024)S(1)} %get-tuple-element.325), channel_id=1, replica_groups=mesh['dp'=4,'wide'=8] {'wide'}, use_global_device_ids=true, to_apply=%region_26.27 | all-reduce | flops 2048 | bytes 16384 | tf_op jit(solution)/shard_map/psum | solution.py:182
  915.2 18.2 %collective-permute-done.23 = bf16[1024,256]{1,0:T(8,128)(2,1)} collective-permute-done((bf16[1024,256]{1,0:T(8,128)(2,1)S(1)}, bf16[1024,256]{1,0:T(8,128)(2,1)}, u32[]{:S(2)}, u32[]{:S(2)}) %collective-permute-start.23) | collective-permute-done | bytes 524320 | tf_op jit(solution)/shard_map/ppermute | solution.py:27
  975.9 30.4 %while.54 = (s32[]{:T(128)}, f32[1024,2,128]{0,2,1:T(8,128)S(1)}, f32[1024,2,128]{0,2,1:T(8,128)}, f32[2,512,2,128]{3,1,2,0:T(8,128)}, s32[2]{0:T(128)S(1)}, /*i...) while((s32[]{:T(128)}, f32[1024,2,128]{0,2,1:T(8,128)S(1)}, ...), condition=%wide.region_31.32_spmd.clone.clone, body=%wide.region_29.31_spmd.clone.sunk.clone | while | flops 1357250560 | bytes 90224648 | solution.py:175
  1091.7 74.4 %reduce-scatter.18.cloned.1.call-done = f32[1024,256]{1,0:T(8,128)} async-done(((f32[1024,2048]{1,0:T(8,128)}), f32[1024,256]{1,0:T(8,128)}) %reduce-scatter.18.cloned.1.call-update) | async-done | bytes 1048592 | tf_op jit(solution)/shard_map/reduce_scatter | solution.py:206
  1167.9 19.7 %all-reduce = (f32[1024]{0:T(1024)S(1)}, f32[1024]{0:T(1024)S(1)}) all-reduce(f32[1024]{0:T(1024)S(1)} %get-tuple-element.324, f32[1024]{0:T(1024)S(1)} %get-tuple-element.323), channel_id=1, replica_groups=mesh['dp'=4,'wide'=8] {'wide'}, use_global_device_ids=true, to_apply=%region_36.37 | all-reduce | flops 2048 | bytes 16384 | tf_op jit(solution)/shard_map/psum | solution.py:182
  1197.0 38.0 %psum.71 = f32[2,4,6]{2,1,0:T(4,128)} all-reduce(f32[2,4,6]{2,1,0:T(4,128)S(1)} %pad_maximum_fusion.3), channel_id=1, replica_groups=mesh['dp'=4,'wide'=8] {'dp','wide'}, use_global_device_ids=true, to_apply=%region_50.51 | all-reduce | flops 48 | bytes 384 | tf_op jit(solution)/shard_map/psum | solution.py:361
  1240.8 74.6 %reduce-scatter.28.cloned.1.call-done = f32[512,1024]{1,0:T(8,128)} async-done(((f32[2048,1024]{1,0:T(8,128)}), f32[512,1024]{1,0:T(8,128)}) %reduce-scatter.28.cloned.1.call-update) | async-done | bytes 2097168 | tf_op jit(solution)/shard_map/reduce_scatter | solution.py:295
  1315.4 74.4 %reduce-scatter.30.cloned.1.call-done = f32[512,1024]{1,0:T(8,128)} async-done(((f32[2048,1024]{1,0:T(8,128)}), f32[512,1024]{1,0:T(8,128)}) %reduce-scatter.30.cloned.1.call-update) | async-done | bytes 2097168 | tf_op jit(solution)/shard_map/reduce_scatter | solution.py:296
  1389.8 34.2 %reduce-scatter.26.cloned.1.call-done = f32[256,512]{1,0:T(8,128)} async-done(((f32[256,2048]{1,0:T(8,128)}), f32[256,512]{1,0:T(8,128)}) %reduce-scatter.26.cloned.1.call-update) | async-done | bytes 524304 | tf_op jit(solution)/shard_map/reduce_scatter | solution.py:374
  1424.0 34.1 %reduce-scatter.24.cloned.1.call-done = f32[512,256]{1,0:T(8,128)} async-done(((f32[2048,256]{1,0:T(8,128)}), f32[512,256]{1,0:T(8,128)}) %reduce-scatter.24.cloned.1.call-update) | async-done | bytes 524304 | tf_op jit(solution)/shard_map/reduce_scatter | solution.py:373
  1458.1 34.1 %reduce-scatter.22.cloned.1.call-done = f32[512,256]{1,0:T(8,128)} async-done(((f32[2048,256]{1,0:T(8,128)}), f32[512,256]{1,0:T(8,128)}) %reduce-scatter.22.cloned.1.call-update) | async-done | bytes 524304 | tf_op jit(solution)/shard_map/reduce_scatter | solution.py:372
  1492.3 34.1 %reduce-scatter.20.cloned.1.call-done = f32[512,256]{1,0:T(8,128)} async-done(((f32[2048,256]{1,0:T(8,128)}), f32[512,256]{1,0:T(8,128)}) %reduce-scatter.20.cloned.1.call-update) | async-done | bytes 524304 | tf_op jit(solution)/shard_map/reduce_scatter | solution.py:371
  (400 shorter events, 491.0 us)
Async XLA Ops:
  7.2 116.2 %all-gather.10.cloned.1.call-start = ((), (), s32[]{:S(2)}) async-start(), calls=%async_computation.12 | async-start | bytes 1310720 | tf_op jit(solution)/shard_map/all_gather | solution.py:240
  7.9 120.3 %all-gather.8.cloned.1.call-start = ((), (), s32[]{:S(2)}) async-start(), calls=%async_computation.11 | async-start | bytes 1310720 | tf_op jit(solution)/shard_map/all_gather | solution.py:239
  8.7 124.8 %all-gather.12.cloned.1.call-start = ((), (), s32[]{:S(2)}) async-start(), calls=%async_computation.13 | async-start | bytes 1310720 | tf_op jit(solution)/shard_map/all_gather | solution.py:241
  9.4 142.5 %all-gather.14.cloned.1.call-start = ((), (), s32[]{:S(2)}) async-start(), calls=%async_computation.14 | async-start | bytes 1310720 | tf_op jit(solution)/shard_map/all_gather | solution.py:242
  45.3 257.8 %reduce-scatter.12.cloned.1.call-start = ((), (), s32[]{:S(2)}) async-start(), calls=%async_computation.15 | async-start | bytes 9437184 | tf_op jit(solution)/shard_map/reduce_scatter | solution.py:190
  88.4 27.6 %collective-permute-start.5 = (bf16[1024,256]{1,0:T(8,128)(2,1)}, bf16[1024,256]{1,0:T(8,128)(2,1)S(1)}, u32[]{:S(2)}, u32[]{:S(2)}) collective-permute-start(bf16[1024,256]{1,0:T(8,128)(2,1)} %collective-permute-done.3), channel_id=1, source_target_pairs={{0,7},{1,0},{2,1},{3,2},{4,3},{5,4},{6,5},{7,6},{8,15},{9,8},{10,9... | collective-permute-start | bytes 1572872 | tf_op jit(solution)/shard_map/ppermute | solution.py:35
  157.9 258.2 %all-gather.16.cloned.1.call-start = ((), (), s32[]{:S(2)}) async-start(), calls=%async_computation.16 | async-start | bytes 5242880 | tf_op jit(solution)/shard_map/all_gather | solution.py:245
  158.4 267.6 %all-gather.18.cloned.1.call-start = ((), (), s32[]{:S(2)}) async-start(), calls=%async_computation.17 | async-start | bytes 5242880 | tf_op jit(solution)/shard_map/all_gather | solution.py:246
  159.2 279.0 %all-gather.20.cloned.1.call-start = ((), (), s32[]{:S(2)}) async-start(), calls=%async_computation.18 | async-start | bytes 5242880 | tf_op jit(solution)/shard_map/all_gather | solution.py:247
  159.9 434.0 %reduce-scatter.14.cloned.1.call-start = ((), (), s32[]{:S(2)}) async-start(), calls=%async_computation.19 | async-start | bytes 9437184 | tf_op jit(solution)/shard_map/reduce_scatter | solution.py:190
  377.9 27.5 %collective-permute-start.12 = (bf16[1024,256]{1,0:T(8,128)(2,1)S(1)}, bf16[1024,256]{1,0:T(8,128)(2,1)S(1)}, u32[]{:S(2)}, u32[]{:S(2)}) collective-permute-start(bf16[1024,256]{1,0:T(8,128)(2,1)S(1)} %collective-permute-done.10), channel_id=1, source_target_pairs={{0,7},{1,0},{2,1},{3,2},{4,3},{5,4},{6,5},{7,6},{8,15},{9,8},{10,9... | collective-permute-start | bytes 1572872 | tf_op jit(solution)/shard_map/ppermute | solution.py:35
  448.8 409.3 %reduce-scatter.16.cloned.1.call-start = ((), (), s32[]{:S(2)}) async-start(), calls=%async_computation.20 | async-start | bytes 9437184 | tf_op jit(solution)/shard_map/reduce_scatter | solution.py:206
  603.0 24.6 %collective-permute-start.15 = (bf16[1024,256]{1,0:T(8,128)(2,1)S(1)}, bf16[1024,256]{1,0:T(8,128)(2,1)S(1)}, u32[]{:S(2)}, u32[]{:S(2)}) collective-permute-start(bf16[1024,256]{1,0:T(8,128)(2,1)S(1)} %get-tuple-element.319), channel_id=1, source_target_pairs={{0,7},{1,0},{2,1},{3,2},{4,3},{5,4},{6,5},{7,6},{8,15},{9,8},{10,9... | collective-permute-start | bytes 1572872 | tf_op jit(solution)/shard_map/ppermute | solution.py:35
  627.6 24.7 %collective-permute-start.17 = (bf16[1024,256]{1,0:T(8,128)(2,1)S(1)}, bf16[1024,256]{1,0:T(8,128)(2,1)S(1)}, u32[]{:S(2)}, u32[]{:S(2)}) collective-permute-start(bf16[1024,256]{1,0:T(8,128)(2,1)S(1)} %collective-permute-done.15), channel_id=1, source_target_pairs={{0,7},{1,0},{2,1},{3,2},{4,3},{5,4},{6,5},{7,6},{8,15},{9,8},{10,9... | collective-permute-start | bytes 1572872 | tf_op jit(solution)/shard_map/ppermute | solution.py:35
  712.6 453.4 %reduce-scatter.18.cloned.1.call-start = ((), (), s32[]{:S(2)}) async-start(), calls=%async_computation.21 | async-start | bytes 9437184 | tf_op jit(solution)/shard_map/reduce_scatter | solution.py:206
  908.8 24.6 %collective-permute-start.23 = (bf16[1024,256]{1,0:T(8,128)(2,1)S(1)}, bf16[1024,256]{1,0:T(8,128)(2,1)}, u32[]{:S(2)}, u32[]{:S(2)}) collective-permute-start(bf16[1024,256]{1,0:T(8,128)(2,1)S(1)} %collective-permute-done.21), channel_id=1, source_target_pairs={{0,1},{1,2},{2,3},{3,4},{4,5},{5,6},{6,7},{7,0},{8,9},{9,10},{10,1... | collective-permute-start | bytes 1572872 | tf_op jit(solution)/shard_map/ppermute | solution.py:27
  911.3 29.2 %collective-permute-start.24 = (bf16[1024,256]{1,0:T(8,128)(2,1)}, bf16[1024,256]{1,0:T(8,128)(2,1)}, u32[]{:S(2)}, u32[]{:S(2)}) collective-permute-start(bf16[1024,256]{1,0:T(8,128)(2,1)} %collective-permute-done.22), channel_id=1, source_target_pairs={{0,7},{1,0},{2,1},{3,2},{4,3},{5,4},{6,5},{7,6},{8,15},{9,8},{10,9... | collective-permute-start | bytes 1572872 | tf_op jit(solution)/shard_map/ppermute | solution.py:35
  1020.8 220.0 %reduce-scatter.32.cloned.1.call-start = ((), (), s32[]{:S(2)}) async-start(), calls=%async_computation.28 | async-start | bytes 10485760 | tf_op jit(solution)/shard_map/reduce_scatter | solution.py:297
  1031.8 283.6 %reduce-scatter.28.cloned.1.call-start = ((), (), s32[]{:S(2)}) async-start(), calls=%async_computation.26 | async-start | bytes 10485760 | tf_op jit(solution)/shard_map/reduce_scatter | solution.py:295
  1042.5 347.3 %reduce-scatter.30.cloned.1.call-start = ((), (), s32[]{:S(2)}) async-start(), calls=%async_computation.27 | async-start | bytes 10485760 | tf_op jit(solution)/shard_map/reduce_scatter | solution.py:296
  1053.6 370.3 %reduce-scatter.26.cloned.1.call-start = ((), (), s32[]{:S(2)}) async-start(), calls=%async_computation.25 | async-start | bytes 2621440 | tf_op jit(solution)/shard_map/reduce_scatter | solution.py:374
  1059.7 398.4 %reduce-scatter.24.cloned.1.call-start = ((), (), s32[]{:S(2)}) async-start(), calls=%async_computation.24 | async-start | bytes 2621440 | tf_op jit(solution)/shard_map/reduce_scatter | solution.py:373
  1064.9 427.4 %reduce-scatter.22.cloned.1.call-start = ((), (), s32[]{:S(2)}) async-start(), calls=%async_computation.23 | async-start | bytes 2621440 | tf_op jit(solution)/shard_map/reduce_scatter | solution.py:372
  1069.9 456.5 %reduce-scatter.20.cloned.1.call-start = ((), (), s32[]{:S(2)}) async-start(), calls=%async_computation.22 | async-start | bytes 2621440 | tf_op jit(solution)/shard_map/reduce_scatter | solution.py:371
  (91 other events, 1597.4 us)
Sparse Core Ops, SparseCore 0:
  9.5 19.4 all-gather.9
  30.6 16.6 all-gather.7
  48.9 16.6 all-gather.11
  67.0 16.6 all-gather.13
  158.0 145.0 reduce-scatter.11
  304.5 33.5 all-gather.15
  339.7 34.4 all-gather.17
  375.7 34.4 all-gather.19
  448.9 145.0 reduce-scatter.13
  712.7 145.2 reduce-scatter.15
  1021.0 145.0 reduce-scatter.17
  1169.0 71.7 reduce-scatter.31
  1244.0 71.3 reduce-scatter.27
  1318.4 71.3 reduce-scatter.29
  1392.8 31.1 reduce-scatter.25
  1426.9 31.1 reduce-scatter.23
  1461.1 31.1 reduce-scatter.21
  1495.2 31.1 reduce-scatter.19
